TPU v7x, 256 devices: a whole 4x4x8 slice. The times are simulated.
256 devices in a mesh: tok: 8 (over x, core), col: 32 (over y, z).
Axes of the slice: x: 4, y: 4, z: 8, core: 2. Of those that a mesh axis runs over, the one named last changes fastest.
Arguments:
- hidden_in: bfloat16 [2048, 36864], P('tok', 'col'), may hold values from -6 to 6
- down_weight: bfloat16 [4608, 36864], P('col', 'tok'), may hold values from -0.046875 to 0.046875
- keep_mask: int32 [4608, 36864], P('col', 'tok'), may hold values 0 or 1
Outputs:
- layer_out: bfloat16 [2048, 4608], P(('tok', 'col'))
- hessian: float32 [4608, 4608], P('col', 'tok')
All inputs are finite; a program needn't handle non-finite values. No bound on the sum of `keep_mask` on one device may be relied on, other than what follows from the above.
Results may differ from a plain program's by a relative error of at most 0.012.
Values may be sent and summed in bfloat16 or wider, within the bound.
A program may use at most 128 MiB of HBM per device.

v0:
```python
import jax
import jax.numpy as jnp
from jax import lax
from jax.sharding import PartitionSpec as P


def laid_out(pieces, dim):
    lengths = list(pieces.shape[1:])
    lengths[dim] *= pieces.shape[0]
    return jnp.moveaxis(pieces, 0, dim).reshape(lengths)


def from_everyone(x, axis):
    size = lax.axis_size(axis)
    return lax.all_to_all(jnp.broadcast_to(x[None], (size, *x.shape)), axis, 0, 0, tiled=True)


def gathered_copies(x, axis, dim):
    return laid_out(from_everyone(x, axis), dim)


def split_up(x, dim, size):
    before, after = (x.shape[:dim], x.shape[dim + 1 :])
    return jnp.moveaxis(x.reshape(*before, size, -1, *after), dim, 0)


def sent_and_summed(x, axis, dim):
    pieces = split_up(x, dim, lax.axis_size(axis))
    arrived = lax.all_to_all(pieces, axis, split_axis=0, concat_axis=0, tiled=True)
    return arrived.astype(jnp.float32).sum(axis=0)


def contract_rows(left, right):
    return lax.dot_general(
        left, right, (((0,), (0,)), ((), ())), preferred_element_type=jnp.float32
    )


def contract_last(left, right):
    return lax.dot_general(
        left, right, (((1,), (1,)), ((), ())), preferred_element_type=jnp.float32
    )


def body(hidden_in, down_weight, keep_mask):
    pruned = down_weight * keep_mask.astype(down_weight.dtype)
    all_features = lax.all_gather(hidden_in, "col", axis=1, tiled=True)
    summed = contract_last(all_features, lax.all_gather(pruned, "tok", axis=1, tiled=True))
    layer_cols = summed.astype(jnp.bfloat16)
    scaling = 2.0 / (layer_cols.shape[0] * lax.axis_size("tok"))
    whole = gathered_copies(layer_cols, "col", 1)
    share_rows = whole.shape[0] // lax.axis_size("col")
    layer_out = lax.dynamic_slice_in_dim(whole, lax.axis_index("col") * share_rows, share_rows, 0)
    hessian_term = contract_rows(layer_cols, whole)
    hessian = sent_and_summed((hessian_term * scaling).astype(jnp.bfloat16), "tok", 1)
    return (layer_out, hessian)


def solution(mesh):
    in_specs = (P("tok", "col"), P("col", "tok"), P("col", "tok"))
    out_specs = (P(("tok", "col"), None), P("col", "tok"))
    return jax.shard_map(body, mesh=mesh, in_specs=in_specs, out_specs=out_specs, check_vma=False)
```

profile of v0, /device:TPU:1, one launch (start us, length us, event | category | flops | bytes accessed | tf_op | source)
XLA Modules:
  0.0 347.3 jit_solution(11855072798509974966)
XLA Ops:
  7.2 0.0 all-gather.3.cloned.1.call-start
  7.2 3.4 convert_multiply_fusion
  10.7 0.0 all-gather.3.cloned.1.call-update
  10.7 0.0 all-gather.5.cloned.1.call-start
  10.7 0.7 all-gather.5.cloned.1.call-update
  11.4 65.1 %all-gather.3.cloned.1.call-done = bf16[144,36864]{1,0:T(8,128)(2,1)} async-done(((bf16[144,4608]{1,0:T(8,128)(2,1)}), bf16[144,36864]{1,0:T(8,128)(2,1)}) %all-gather.3.cloned.1.call-update) | async-done | bytes 10616848 | tf_op jit(solution)/shard_map/all_gather | solution.py:48
  76.6 152.6 %all-gather.5.cloned.1.call-done = bf16[256,36864]{1,0:T(8,128)(2,1)} async-done(((bf16[256,1152]{1,0:T(8,128)(2,1)}), bf16[256,36864]{1,0:T(8,128)(2,1)}) %all-gather.5.cloned.1.call-update) | async-done | bytes 18874384 | tf_op jit(solution)/shard_map/all_gather | solution.py:47
  229.1 12.8 %convolution_convert_fusion = bf16[144,256]{1,0:T(8,128)(2,1)S(1)} fusion(bf16[144,36864]{1,0:T(8,128)(2,1)} %all-gather.3.cloned.1.call-done, bf16[256,36864]{1,0:T(8,128)(2,1)} %all-gather.5.cloned.1.call-done), kind=kOutput, calls=%fused_computation.5 | convolution fusion | flops 2717945856 | bytes 29564928 | tf_op jit(solution)/shard_map/dot_general | solution.py:40
  241.9 0.2 broadcast_in_dim.2
  242.1 58.9 %all_to_all.10 = bf16[32,256,144]{1,2,0:T(8,128)(2,1)S(1)} all-to-all(bf16[32,256,144]{1,2,0:T(8,128)(2,1)S(1)} %broadcast_in_dim.2), channel_id=1, replica_groups=mesh['tok'=8,'col'=32] {'col'}, dimensions={0} | all-to-all | bytes 4718592 | tf_op jit(solution)/shard_map/all_to_all | solution.py:15
  300.9 2.0 fusion
  303.0 3.7 %reshape.12 = bf16[144,8,576]{2,1,0:T(8,128)(2,1)} reshape(bf16[144,4608]{1,0:T(8,128)(2,1)} %fusion) | data formatting | bytes 2654208 | tf_op jit(solution)/shard_map/reshape | solution.py:24
  306.7 2.7 copy.10
  309.4 9.1 %all-to-all-start.1 = ((bf16[8,144,576]{2,1,0:T(8,128)(2,1)}), bf16[8,144,576]{2,1,0:T(8,128)(2,1)}, u32[]{:S(2)}, u32[]{:S(2)}) async-start(bf16[8,144,576]{2,1,0:T(8,128)(2,1)} %bitcast.13), calls=%async_computation.1 | async-start | bytes 2949120 | tf_op jit(solution)/shard_map/all_to_all | solution.py:29
  318.4 0.4 constant_dynamic-slice_fusion
  318.8 1.0 copy.8
  319.8 18.3 %all-to-all-done.1 = bf16[8,144,576]{2,1,0:T(8,128)(2,1)} async-done(((bf16[8,144,576]{2,1,0:T(8,128)(2,1)}), bf16[8,144,576]{2,1,0:T(8,128)(2,1)}, u32[]{:S(2)}, u32[]{:S(2)}) %all-to-all-start.1) | async-done | bytes 1327136 | tf_op jit(solution)/shard_map/all_to_all | solution.py:29
  338.1 2.4 convert_reduce_fusion
Async XLA Ops:
  7.2 69.4 %all-gather.3.cloned.1.call-start = ((), (), s32[]{:S(2)}) async-start(), calls=%async_computation.2 | async-start | bytes 11943936 | tf_op jit(solution)/shard_map/all_gather | solution.py:48
  10.7 218.5 %all-gather.5.cloned.1.call-start = ((), (), s32[]{:S(2)}) async-start(), calls=%async_computation.3 | async-start | bytes 19464192 | tf_op jit(solution)/shard_map/all_gather | solution.py:47
  309.4 28.7 %all-to-all-start.1 = ((bf16[8,144,576]{2,1,0:T(8,128)(2,1)}), bf16[8,144,576]{2,1,0:T(8,128)(2,1)}, u32[]{:S(2)}, u32[]{:S(2)}) async-start(bf16[8,144,576]{2,1,0:T(8,128)(2,1)} %bitcast.13), calls=%async_computation.1 | async-start | bytes 2949120 | tf_op jit(solution)/shard_map/all_to_all | solution.py:29
Sparse Core Ops, SparseCore 0:
  10.8 65.7 all-gather.2
  79.3 149.8 all-gather.4
where the time goes:
time: 348 us; the launch traced here: 347 us
  waiting for transfers between devices  237 us (68%)
  blocking collectives  58.9 us (17%)
  matrix products  14.8 us (4%)
  between operations  14.1 us (4%)
  starting transfers between devices  9.16 us (3%)
  local copies, waits for them, and re-layouts  7.93 us (2%)
  other arithmetic  5.8 us (2%)
    all_gather x1, waiting for transfers between devices, body(): all_features = lax.all_gather(hidden_in, 'col', axis=1, tiled=True)  153 us
    all_gather x1, waiting for transfers between devices, body(): lax.all_gather(pruned, 'tok', axis=1, tiled=True)  65.1 us
    all_to_all x1, blocking collectives, from_everyone(): lax.all_to_all(jnp.broadcast_to(x[None], (size, *x.shape)), axis, 0, 0, t...  58.9 us
    all_to_all x1, waiting for transfers between devices, sent_and_summed(): lax.all_to_all(pieces, axis, split_axis=0, concat_axis=0, tiled=True)  18.3 us
    dot_general x1, matrix products, contract_last(): lax.dot_general(left, right, (((1,), (1,)), ((), ())), preferred_element_...  12.8 us
    all_to_all x1, starting transfers between devices, sent_and_summed(): lax.all_to_all(pieces, axis, split_axis=0, concat_axis=0, tiled=True)  9.08 us
  transfers between devices with their start and end apart: 3, of which 3 were waited for; matrix products, arithmetic and copies ran while one was open for 0% of the time, Pallas kernels for 0%

commit v1 on v0

--- a/solution.py
+++ b/solution.py
@@ -2,6 +2,19 @@
 import jax.numpy as jnp
 from jax import lax
 from jax.sharding import PartitionSpec as P
+from jax.lax import all_to_all, axis_size
+
+
+def change_the_screen(my_data):
+    bus_axis = "tok"
+    many = axis_size(bus_axis)
+    return all_to_all(
+        jnp.tile(my_data, [many if num == 1 else 1 for num in range(my_data.ndim)]),
+        axis_name=bus_axis,
+        split_axis=1,
+        concat_axis=1,
+        tiled=True,
+    )
 
 
 def laid_out(pieces, dim):
@@ -45,7 +58,7 @@
 def body(hidden_in, down_weight, keep_mask):
     pruned = down_weight * keep_mask.astype(down_weight.dtype)
     all_features = lax.all_gather(hidden_in, "col", axis=1, tiled=True)
-    summed = contract_last(all_features, lax.all_gather(pruned, "tok", axis=1, tiled=True))
+    summed = contract_last(all_features, change_the_screen(pruned))
     layer_cols = summed.astype(jnp.bfloat16)
     scaling = 2.0 / (layer_cols.shape[0] * lax.axis_size("tok"))
     whole = gathered_copies(layer_cols, "col", 1)

time: 348 us -> 283 us (0.81)
  waiting for transfers between devices: 237 us -> 38.7 us
  blocking collectives: 58.9 us -> 184 us
  local copies, waits for them, and re-layouts: 7.93 us -> 17.5 us
    all_gather x1, waiting for transfers between devices: 153 us -> 19.8 us  [body(): all_features = lax.all_gather(hidden_in, 'col', axis=1, tiled=True)]
    all_to_all x0 -> x1, blocking collectives: none -> 125 us  [change_the_screen(): all_to_all(jnp.tile(my_data, [many if num == 1 else 1 for num in range(my...]
    all_gather x1 -> x0, waiting for transfers between devices: 65.1 us -> none  [body(): lax.all_gather(pruned, 'tok', axis=1, tiled=True)]
    another operation x0 -> x1, local copies, waits for them, and re-layouts: none -> 4.87 us  [change_the_screen(): jnp.tile(my_data, [many if num == 1 else 1 for num in range(my_data.ndim)])]
    all_to_all x0 -> x1, local copies, waits for them, and re-layouts: none -> 4.73 us  [change_the_screen(): all_to_all(jnp.tile(my_data, [many if num == 1 else 1 for num in range(my...]
  transfers between devices with their start and end apart: 3 -> 2, of which waited for: 3 -> 2; matrix products, arithmetic and copies ran while one was open for 0% -> 5% of each run, Pallas kernels for 0% -> 0%
where the time goes in v1:
time: 283 us
  blocking collectives  184 us (65%)
  waiting for transfers between devices  38.7 us (14%)
  local copies, waits for them, and re-layouts  17.5 us (6%)
  matrix products  14.8 us (5%)
  between operations  14.1 us (5%)
  starting transfers between devices  9.12 us (3%)
  other arithmetic  4.69 us (2%)
    all_to_all x1, blocking collectives, change_the_screen(): all_to_all(jnp.tile(my_data, [many if num == 1 else 1 for num in range(my...  125 us
    all_to_all x1, blocking collectives, from_everyone(): lax.all_to_all(jnp.broadcast_to(x[None], (size, *x.shape)), axis, 0, 0, t...  58.9 us
    all_gather x1, waiting for transfers between devices, body(): all_features = lax.all_gather(hidden_in, 'col', axis=1, tiled=True)  19.8 us
    all_to_all x1, waiting for transfers between devices, sent_and_summed(): lax.all_to_all(pieces, axis, split_axis=0, concat_axis=0, tiled=True)  18.3 us
    dot_general x1, matrix products, contract_last(): lax.dot_general(left, right, (((1,), (1,)), ((), ())), preferred_element_...  12.8 us
    all_to_all x1, starting transfers between devices, sent_and_summed(): lax.all_to_all(pieces, axis, split_axis=0, concat_axis=0, tiled=True)  9.08 us
    reshape x2, local copies, waits for them, and re-layouts, split_up(): return jnp.moveaxis(x.reshape(*before, size, -1, *after), dim, 0)  6.41 us
  transfers between devices with their start and end apart: 2, of which 2 were waited for; matrix products, arithmetic and copies ran while one was open for 5% of the time, Pallas kernels for 0%

profile of v1, /device:TPU:1, one launch (start us, length us, event | category | flops | bytes accessed | tf_op | source)
XLA Modules:
  0.0 282.5 jit_solution(15644688889364216236)
XLA Ops:
  7.2 0.0 all-gather.2.cloned.1.call-start
  7.2 0.7 all-gather.2.cloned.1.call-update
  7.9 2.3 convert_multiply_fusion
  10.2 4.9 %tile.2 = bf16[144,8,4608]{2,0,1:T(8,128)(2,1)} broadcast(bf16[144,4608]{1,0:T(8,128)(2,1)S(1)} %convert_multiply_fusion), dimensions={0,2} | broadcast | bytes 11943936 | tf_op jit(solution)/shard_map/tile | solution.py:12
  15.1 124.8 %all_to_all.19 = bf16[144,8,4608]{2,0,1:T(8,128)(2,1)S(1)} all-to-all(bf16[144,8,4608]{2,0,1:T(8,128)(2,1)} %tile.2), channel_id=1, replica_groups=mesh['tok'=8,'col'=32] {'tok'}, dimensions={1} | all-to-all | bytes 21233664 | tf_op jit(solution)/shard_map/all_to_all | solution.py:11
  139.9 4.7 %copy.12 = bf16[8,18,8,4608]{3,2,0,1:T(8,128)(2,1)} copy(bf16[8,18,8,4608]{3,2,1,0:T(8,128)(2,1)S(1)} %bitcast.14) | data formatting | bytes 21233664 | tf_op jit(solution)/shard_map/all_to_all | solution.py:11
  144.6 19.8 %all-gather.2.cloned.1.call-done = bf16[256,36864]{1,0:T(8,128)(2,1)} async-done(((bf16[256,1152]{1,0:T(8,128)(2,1)}), bf16[256,36864]{1,0:T(8,128)(2,1)}) %all-gather.2.cloned.1.call-update) | async-done | bytes 18874384 | tf_op jit(solution)/shard_map/all_gather | solution.py:60
  164.4 12.8 %convolution_convert_fusion = bf16[144,256]{1,0:T(8,128)(2,1)S(1)} fusion(bf16[144,36864]{1,0:T(8,128)(2,1)} %bitcast.13, bf16[256,36864]{1,0:T(8,128)(2,1)} %all-gather.2.cloned.1.call-done), kind=kOutput, calls=%fused_computation.5 | convolution fusion | flops 2717945856 | bytes 29564928 | tf_op jit(solution)/shard_map/dot_general | solution.py:53
  177.2 0.2 broadcast_in_dim.2
  177.3 58.9 %all_to_all.20 = bf16[32,256,144]{1,2,0:T(8,128)(2,1)S(1)} all-to-all(bf16[32,256,144]{1,2,0:T(8,128)(2,1)S(1)} %broadcast_in_dim.2), channel_id=1, replica_groups=mesh['tok'=8,'col'=32] {'col'}, dimensions={0} | all-to-all | bytes 4718592 | tf_op jit(solution)/shard_map/all_to_all | solution.py:28
  236.2 2.0 fusion
  238.2 3.8 %reshape.19 = bf16[144,8,576]{2,1,0:T(8,128)(2,1)} reshape(bf16[144,4608]{1,0:T(8,128)(2,1)} %fusion) | data formatting | bytes 2654208 | tf_op jit(solution)/shard_map/reshape | solution.py:37
  242.0 2.7 copy.14
  244.6 9.1 %all-to-all-start.2 = ((bf16[8,144,576]{2,1,0:T(8,128)(2,1)}), bf16[8,144,576]{2,1,0:T(8,128)(2,1)}, u32[]{:S(2)}, u32[]{:S(2)}) async-start(bf16[8,144,576]{2,1,0:T(8,128)(2,1)} %bitcast.17), calls=%async_computation.2 | async-start | bytes 2949120 | tf_op jit(solution)/shard_map/all_to_all | solution.py:42
  253.7 0.4 constant_dynamic-slice_fusion
  254.1 1.0 copy.11
  255.1 18.3 %all-to-all-done.2 = bf16[8,144,576]{2,1,0:T(8,128)(2,1)} async-done(((bf16[8,144,576]{2,1,0:T(8,128)(2,1)}), bf16[8,144,576]{2,1,0:T(8,128)(2,1)}, u32[]{:S(2)}, u32[]{:S(2)}) %all-to-all-start.2) | async-done | bytes 1327136 | tf_op jit(solution)/shard_map/all_to_all | solution.py:42
  273.3 2.4 convert_reduce_fusion
Async XLA Ops:
  7.2 157.2 %all-gather.2.cloned.1.call-start = ((), (), s32[]{:S(2)}) async-start(), calls=%async_computation.3 | async-start | bytes 19464192 | tf_op jit(solution)/shard_map/all_gather | solution.py:60
  244.6 28.7 %all-to-all-start.2 = ((bf16[8,144,576]{2,1,0:T(8,128)(2,1)}), bf16[8,144,576]{2,1,0:T(8,128)(2,1)}, u32[]{:S(2)}, u32[]{:S(2)}) async-start(bf16[8,144,576]{2,1,0:T(8,128)(2,1)} %bitcast.17), calls=%async_computation.2 | async-start | bytes 2949120 | tf_op jit(solution)/shard_map/all_to_all | solution.py:42
Sparse Core Ops, SparseCore 0:
  10.7 153.6 all-gather.1
